TPU v7x, 32 devices: a 4x4x1 block of a 4x4x8 slice. The times are simulated.
32 devices in a mesh: dp: 1 (over z), tp: 4 (over y), sp: 8 (over x, core).
Axes of the slice: x: 4, y: 4, z: 1, core: 2. Of those that a mesh axis runs over, the one named last changes fastest.
The devices are a block of a 4x4x8 slice.
Arguments:
- hidden: bfloat16 [32768, 2048], P(('dp', 'sp'))
- w_query: bfloat16 [2048, 2048], P(None, 'tp')
- w_key: bfloat16 [2048, 2048], P(None, 'tp')
- w_value: bfloat16 [2048, 2048], P(None, 'tp')
- w_out: bfloat16 [2048, 2048], P('tp')
- branch_bias: float32 [4, 8], replicated
Outputs:
- output: bfloat16 [32768, 2048], P(('dp', 'sp'), 'tp')
All inputs are finite; a program needn't handle non-finite values.
Results may differ from a plain program's by a relative error of at most 0.00338052.
Values are sent between devices in bfloat16 or wider.
A program may use at most 768 MiB of HBM per device.

v0:
```python
import jax
import jax.numpy as jnp
from jax import lax
from jax.sharding import PartitionSpec as P

SEG_BASE = 2048


def attend(q_sel, k_sel, v_sel, logit_scale):
    logits = jnp.einsum('hasd,hatd->hast', q_sel, k_sel, preferred_element_type=jnp.float32) * logit_scale
    row_max = jnp.max(logits, axis=-1, keepdims=True)
    weights = jnp.exp(logits - row_max)
    row_sum = jnp.sum(weights, axis=-1, keepdims=True)
    numer_sum = jnp.einsum('hast,hatd->hasd', weights.astype(jnp.bfloat16), v_sel, preferred_element_type=jnp.float32)
    return numer_sum / row_sum, (row_max + jnp.log(row_sum))[..., 0]


def solution(mesh):
    seq_size = mesh.shape['sp']
    head_groups = mesh.shape['tp']

    def device_fn(hidden, w_query, w_key, w_value, w_out, branch_bias):
        tokens, model_width = hidden.shape
        num_branches, num_heads = branch_bias.shape
        head_dim = model_width // num_heads
        local_heads = num_heads // head_groups
        logit_scale = head_dim ** -0.5
        head_start = lax.axis_index('tp') * local_heads
        head_ids = head_start + jnp.arange(local_heads)
        bias_local = lax.dynamic_slice_in_dim(branch_bias, head_start, local_heads, axis=1)

        def project(weight):
            return jnp.dot(hidden, weight, preferred_element_type=jnp.float32).astype(jnp.bfloat16).reshape(tokens, local_heads, head_dim)

        q_loc = project(w_query)
        k_loc = project(w_key)
        v_loc = project(w_value)
        for branch in range(num_branches):
            value_a8 = 2 ** branch
            seg_len = SEG_BASE * value_a8
            kept_rows = tokens // value_a8
            phase_ok = head_ids[:, None] % value_a8 == jnp.arange(value_a8)[None, :]
            phase_bf = phase_ok.astype(jnp.bfloat16)
            phase_f = phase_ok.astype(jnp.float32)

            def pick_rows(source):
                split_rows = source.reshape(kept_rows, value_a8, local_heads, head_dim)
                return jnp.einsum('sihd,hi->hsd', split_rows, phase_bf, preferred_element_type=jnp.float32).astype(jnp.bfloat16)

            q_sel = pick_rows(q_loc)
            k_sel = pick_rows(k_loc)
            v_sel = pick_rows(v_loc)
            if seg_len <= tokens:
                seg_shape = (local_heads, tokens // seg_len, SEG_BASE, head_dim)
                attn_out, log_norm = attend(q_sel.reshape(seg_shape), k_sel.reshape(seg_shape), v_sel.reshape(seg_shape), logit_scale)
            else:
                group_len = seg_len // tokens
                k_parts = [k_sel]
                v_parts = [v_sel]
                for shift_by in range(1, group_len):
                    pairs_list = [(source_dev, (source_dev // group_len) * group_len + (source_dev + shift_by) % group_len) for source_dev in range(seq_size)]
                    k_parts.append(lax.ppermute(k_sel, 'sp', pairs_list))
                    v_parts.append(lax.ppermute(v_sel, 'sp', pairs_list))
                k_seg = jnp.concatenate(k_parts, axis=1)[:, None]
                v_seg = jnp.concatenate(v_parts, axis=1)[:, None]
                attn_out, log_norm = attend(q_sel[:, None], k_seg, v_seg, logit_scale)
            out_full = jnp.einsum('hsd,hi->sihd', attn_out.reshape(local_heads, kept_rows, head_dim), phase_f).reshape(tokens, local_heads, head_dim)
            lse_full = jnp.einsum('hs,hi->sih', log_norm.reshape(local_heads, kept_rows), phase_f).reshape(tokens, local_heads)
            mask_full = jnp.broadcast_to(phase_ok.T[None], (kept_rows, value_a8, local_heads)).reshape(tokens, local_heads)
            branch_score = jnp.where(mask_full, lse_full + bias_local[branch][None, :], -jnp.inf)
            if branch == 0:
                run_num = out_full
                run_max = branch_score
                run_den = jnp.ones_like(branch_score)
            else:
                new_max = jnp.maximum(run_max, branch_score)
                keep_old = jnp.exp(run_max - new_max)
                take_new = jnp.exp(branch_score - new_max)
                run_num = run_num * keep_old[..., None] + out_full * take_new[..., None]
                run_den = run_den * keep_old + take_new
                run_max = new_max
        combined = (run_num / run_den[..., None]).astype(jnp.bfloat16).reshape(tokens, local_heads * head_dim)
        part_out = jnp.dot(combined, w_out, preferred_element_type=jnp.float32)
        reduced = lax.psum_scatter(part_out, 'tp', scatter_dimension=1, tiled=True)
        return reduced.astype(jnp.bfloat16)

    return jax.shard_map(device_fn, mesh=mesh, in_specs=(P(('dp', 'sp'), None), P(None, 'tp'), P(None, 'tp'), P(None, 'tp'), P('tp', None), P(None, None)), out_specs=P(('dp', 'sp'), 'tp'), check_vma=False)
```

profile of v0, /device:TPU:97, one launch (start us, length us, event | category | flops | bytes accessed | tf_op | source)
XLA Modules:
  0.0 788.1 jit_solution(902496593467112297)
XLA Ops:
  7.3 14.5 %convolution_convert_fusion = bf16[4096,512]{0,1:T(8,128)(2,1)} fusion(bf16[4096,2048]{1,0:T(8,128)(2,1)} %param.6, bf16[2048,512]{1,0:T(8,128)(2,1)} %param.9), kind=kOutput, calls=%fused_computation.37 | convolution fusion | flops 8592031744 | bytes 23068672 | tf_op jit(solution)/shard_map/dot_general | solution.py:33
  28.2 7.0 reshape_reshape.38
  42.7 13.9 %convolution_convert_fusion.1 = bf16[4096,512]{0,1:T(8,128)(2,1)} fusion(bf16[4096,2048]{1,0:T(8,128)(2,1)} %param.6, bf16[2048,512]{1,0:T(8,128)(2,1)S(1)} %copy-done.12), kind=kOutput, calls=%fused_computation.38 | convolution fusion | flops 8592031744 | bytes 23068672 | tf_op jit(solution)/shard_map/dot_general | solution.py:33
  63.1 7.0 reshape_reshape.37
  77.7 7.0 reshape_reshape.34
  84.6 14.4 %convolution_convert_fusion.2 = bf16[4096,512]{0,1:T(8,128)(2,1)} fusion(bf16[4096,2048]{1,0:T(8,128)(2,1)} %param.6, bf16[2048,512]{1,0:T(8,128)(2,1)} %param.7), kind=kOutput, calls=%fused_computation.39 | convolution fusion | flops 8592031744 | bytes 23068672 | tf_op jit(solution)/shard_map/dot_general | solution.py:33
  105.6 6.9 reshape_reshape.36
  112.5 6.9 reshape_reshape.33
  119.4 7.0 reshape_reshape.35
  126.4 6.9 reshape_reshape.31
  133.3 6.9 reshape_reshape.30
  140.2 6.9 reshape_reshape.32
  163.8 11.8 %fusion.48 = bf16[2,1,2048,256]{3,1,2,0:T(2,128)(2,1)} fusion(pred[2,2,1,1]{1,2,3,0:T(4,128)(4,1)S(1)} %copy.68, bf16[2048,2,2,256]{3,2,1,0:T(2,128)(2,1)} %reshape_reshape.31), kind=kOutput, calls=%fused_computation.63 | convolution fusion | flops 4194304 | bytes 6291460 | tf_op jit(solution)/shard_map/sihd,hi->hsd/dot_general | solution.py:48
  175.6 8.8 %fusion.50 = bf16[2,1,2048,256]{3,1,2,0:T(2,128)(2,1)S(1)} fusion(pred[2,2,1,1]{1,2,3,0:T(4,128)(4,1)S(1)} %copy.68, bf16[2048,2,2,256]{3,2,1,0:T(2,128)(2,1)S(1)} %copy-done.2), kind=kOutput, calls=%fused_computation.65 | convolution fusion | flops 4194304 | bytes 6291460 | tf_op jit(solution)/shard_map/sihd,hi->hsd/dot_general | solution.py:48
  190.5 15.4 %multiply_reduce_fusion.1 = (f32[2,2048]{1,0:T(2,128)S(1)}, f32[2,2048,2048]{1,2,0:T(8,128)}) fusion(bf16[2,1,2048,256]{3,1,2,0:T(2,128)(2,1)} %fusion.48, bf16[2,1,2048,256]{3,1,2,0:T(2,128)(2,1)S(1)} %fusion.50), kind=kOutput, calls=%fused_computation.8 | convolution fusion | flops 4311740416 | bytes 37765120 | tf_op jit(solution)/shard_map/hasd,hatd->hast/dot_general | solution.py:10
  205.8 13.5 %fusion.7 = f32[2,2048]{1,0:T(2,128)S(1)} fusion(f32[2,2048,2048]{1,2,0:T(8,128)} %get-tuple-element.28, f32[2,2048]{1,0:T(2,128)S(1)} %get-tuple-element.27), kind=kLoop, calls=%fused_computation.10 | loop fusion | flops 25161728 | bytes 33587200 | tf_op jit(solution)/shard_map/reduce_sum | solution.py:13
  219.4 17.8 %fusion.52 = f32[2,2048,256]{2,1,0:T(8,128)} fusion(f32[2,2048,2048]{1,2,0:T(8,128)} %get-tuple-element.28, f32[2,2048]{1,0:T(2,128)S(1)} %get-tuple-element.27, bf16[2,1,2048,256]{3,1,2,0:T(2,128)(2,1)} %fusion.46, f32[2,2048]{1,0:T(2,128)S(1)} %fusion.7), kind=kOutput, calls=%fused_computation.67 | convolution fusion | flops 4321181696 | bytes 39878656 | tf_op jit(solution)/shard_map/hast,hatd->hasd/dot_general | solution.py:14
  237.2 8.8 %copy.52 = f32[2,2048,256]{2,0,1:T(2,128)} copy(f32[2,2048,256]{2,1,0:T(8,128)} %fusion.52) | data formatting | bytes 8388608 | tf_op jit(solution)/shard_map/div | solution.py:15
  255.3 8.9 %copy.53 = f32[4096,512]{0,1:T(8,128)} copy(f32[4096,512]{1,0:T(8,128)} %bitcast.176) | data formatting | bytes 16777216 | tf_op jit(solution)/shard_map/reshape | solution.py:67
  283.2 26.4 %multiply_reduce_fusion = (f32[2,2,2048]{2,1,0:T(2,128)S(1)}, f32[2,2,2048,2048]{2,3,1,0:T(8,128)}) fusion(bf16[2,2,2048,256]{3,2,1,0:T(8,128)(2,1)} %bitcast.179, bf16[2,2,2048,256]{3,2,1,0:T(8,128)(2,1)} %bitcast.180), kind=kOutput, calls=%fused_computation.1 | convolution fusion | flops 8623480832 | bytes 75530240 | tf_op jit(solution)/shard_map/hasd,hatd->hast/dot_general | solution.py:10
  309.6 21.4 %fusion = f32[2,2,2048]{2,1,0:T(2,128)S(1)} fusion(f32[2,2,2048,2048]{2,3,1,0:T(8,128)} %get-tuple-element.30, f32[2,2,2048]{2,1,0:T(2,128)S(1)} %get-tuple-element.29), kind=kLoop, calls=%fused_computation.2 | loop fusion | flops 50323456 | bytes 67174400 | tf_op jit(solution)/shard_map/reduce_sum | solution.py:13
  331.0 28.6 %fusion.27 = f32[2,2,2048,256]{3,2,1,0:T(8,128)} fusion(bf16[2,2,2048,256]{3,2,1,0:T(8,128)(2,1)} %bitcast.187, f32[2,2,2048,2048]{2,3,1,0:T(8,128)} %get-tuple-element.30, f32[2,2,2048]{2,1,0:T(2,128)S(1)} %get-tuple-element.29, f32[2,2,2048]{2,1,0:T(2,128)S(1)} %fusion), kind=kOutput, calls=%fused_computation.40 | convolution fusion | flops 8642363392 | bytes 79757312 | tf_op jit(solution)/shard_map/hast,hatd->hasd/dot_general | solution.py:14
  359.6 8.9 %copy.46 = f32[2,1,4096,256]{2,3,0,1:T(8,128)} copy(f32[2,1,4096,256]{3,2,0,1:T(8,128)} %bitcast.184) | data formatting | bytes 16777216 | tf_op jit(solution)/shard_map/hsd,hi->sihd/dot_general | solution.py:67
  393.5 9.3 %multiply_bitcast_fusion = f32[512,8,2,256]{3,2,1,0:T(2,128)} fusion(f32[2,512,256]{2,0,1:T(2,128)} %copy.64, f32[2,8]{0,1:T(8,128)S(1)} %copy-done.6), kind=kLoop, calls=%fused_computation.29 | loop fusion | flops 2097152 | bytes 9437248
  402.8 7.6 copy.91
  410.4 8.9 %copy.65 = f32[4096,512]{0,1:T(8,128)} copy(f32[4096,512]{1,0:T(8,128)} %bitcast.177) | data formatting | bytes 16777216 | tf_op jit(solution)/shard_map/reshape | solution.py:67
  436.7 7.8 broadcast_multiply_fusion
  444.4 7.6 copy.90
  452.0 8.9 %copy.59 = f32[4096,512]{0,1:T(8,128)} copy(f32[4096,512]{1,0:T(8,128)} %bitcast.178) | data formatting | bytes 16777216 | tf_op jit(solution)/shard_map/reshape | solution.py:67
  462.2 12.8 %fusion.24 = bf16[4096,512]{0,1:T(8,128)(2,1)S(1)} fusion(f32[4096,512]{0,1:T(8,128)} %copy.65, f32[4096,512]{0,1:T(8,128)} %copy.59, f32[4096,512]{0,1:T(8,128)} %copy.53, f32[2,1,4096,256]{2,3,0,1:T(8,128)} %copy.46, f32[4096,2]{0,1:T(2,128)S(1)} %get-tuple-element.5, f32[4096,2]{0,1:T(2,128)S(1)} %get-tuple-element.11, ...), kind=kLoop, calls=%fused_computation.33 | loop fusion | flops 23068672 | bytes 37978112 | tf_op jit(solution)/shard_map/convert_element_type | solution.py:82
  475.1 15.6 %fusion.107 = f32[4096,2048]{1,0:T(8,128)} fusion(bf16[4096,512]{0,1:T(8,128)(2,1)S(1)} %fusion.24, bf16[512,2048]{1,0:T(8,128)(2,1)S(1)} %copy-done), kind=kOutput, calls=%fused_computation.154 | convolution fusion | flops 8589934592 | bytes 39845888 | tf_op jit(solution)/shard_map/dot_general | solution.py:83
  490.7 284.3 %reduce-scatter.2.cloned.1.call-done = f32[4096,512]{1,0:T(8,128)} async-done(((f32[4096,2048]{1,0:T(8,128)}), f32[4096,512]{1,0:T(8,128)}) %reduce-scatter.2.cloned.1.call-update) | async-done | bytes 8388624 | tf_op jit(solution)/shard_map/reduce_scatter | solution.py:84
  (109 shorter events, 135.7 us)
Async XLA Ops:
  6.5 468.5 %copy-start = (bf16[512,2048]{1,0:T(8,128)(2,1)S(1)}, bf16[512,2048]{1,0:T(8,128)(2,1)}, u32[]{:S(2)}) copy-start(bf16[512,2048]{1,0:T(8,128)(2,1)} %param.10) | copy-start | bytes 6291460
  6.6 768.5 %reduce-scatter.2.cloned.1.call-start = ((), (), s32[]{:S(2)}) async-start(), calls=%async_computation.1 | async-start | bytes 41943040 | tf_op jit(solution)/shard_map/reduce_scatter | solution.py:84
  35.2 7.6 copy-start.12
  39.6 348.4 %collective-permute-start.7 = (bf16[2,512,256]{2,1,0:T(8,128)(2,1)}, bf16[2,512,256]{2,1,0:T(8,128)(2,1)}, u32[]{:S(2)}, u32[]{:S(2)}) collective-permute-start(bf16[2,512,256]{2,1,0:T(8,128)(2,1)} %bitcast.172), channel_id=1, source_target_pairs={{0,3},{1,0},{2,1},{3,2},{4,7},{5,4},{6,5},{7,6},{8,11},{9,8},{10,9... | collective-permute-start | bytes 1572872 | tf_op jit(solution)/shard_map/ppermute | solution.py:63
  42.0 346.1 %collective-permute-start.6 = (bf16[2,512,256]{2,1,0:T(8,128)(2,1)}, bf16[2,512,256]{2,1,0:T(8,128)(2,1)}, u32[]{:S(2)}, u32[]{:S(2)}) collective-permute-start(bf16[2,512,256]{2,1,0:T(8,128)(2,1)} %bitcast.172), channel_id=1, source_target_pairs={{0,2},{1,3},{2,0},{3,1},{4,6},{5,7},{6,4},{7,5},{8,10},{9,11},{10,... | collective-permute-start | bytes 1572872 | tf_op jit(solution)/shard_map/ppermute | solution.py:63
  74.4 308.3 %collective-permute-start.4 = (bf16[2,512,256]{2,1,0:T(8,128)(2,1)}, bf16[2,512,256]{2,1,0:T(8,128)(2,1)}, u32[]{:S(2)}, u32[]{:S(2)}) collective-permute-start(bf16[2,512,256]{2,1,0:T(8,128)(2,1)} %bitcast.173), channel_id=1, source_target_pairs={{0,3},{1,0},{2,1},{3,2},{4,7},{5,4},{6,5},{7,6},{8,11},{9,8},{10,9... | collective-permute-start | bytes 1572872 | tf_op jit(solution)/shard_map/ppermute | solution.py:62
  74.8 307.9 %collective-permute-start.3 = (bf16[2,512,256]{2,1,0:T(8,128)(2,1)}, bf16[2,512,256]{2,1,0:T(8,128)(2,1)}, u32[]{:S(2)}, u32[]{:S(2)}) collective-permute-start(bf16[2,512,256]{2,1,0:T(8,128)(2,1)} %bitcast.173), channel_id=1, source_target_pairs={{0,2},{1,3},{2,0},{3,1},{4,6},{5,7},{6,4},{7,5},{8,10},{9,11},{10,... | collective-permute-start | bytes 1572872 | tf_op jit(solution)/shard_map/ppermute | solution.py:62
  75.9 307.3 %collective-permute-start.2 = (bf16[2,512,256]{2,1,0:T(8,128)(2,1)}, bf16[2,512,256]{2,1,0:T(8,128)(2,1)}, u32[]{:S(2)}, u32[]{:S(2)}) collective-permute-start(bf16[2,512,256]{2,1,0:T(8,128)(2,1)} %bitcast.173), channel_id=1, source_target_pairs={{0,1},{1,2},{2,3},{3,0},{4,5},{5,6},{6,7},{7,4},{8,9},{9,10},{10,1... | collective-permute-start | bytes 1572872 | tf_op jit(solution)/shard_map/ppermute | solution.py:62
  153.5 5.8 copy-start.13
  153.5 5.8 copy-start.4
  163.8 11.8 %copy-start.2 = (bf16[2048,2,2,256]{3,2,1,0:T(2,128)(2,1)S(1)}, bf16[2048,2,2,256]{3,2,1,0:T(2,128)(2,1)}, u32[]{:S(2)}) copy-start(bf16[2048,2,2,256]{3,2,1,0:T(2,128)(2,1)} %reshape_reshape.30) | copy-start | bytes 12582916
  175.5 8.8 %copy-start.3 = (bf16[2048,2,2,256]{3,2,1,0:T(2,128)(2,1)S(1)}, bf16[2048,2,2,256]{3,2,1,0:T(2,128)(2,1)}, u32[]{:S(2)}) copy-start(bf16[2048,2,2,256]{3,2,1,0:T(2,128)(2,1)} %reshape_reshape.32) | copy-start | bytes 12582916
  359.6 9.0 %copy-start.8 = (pred[2,2]{0,1:T(4,128)(4,1)S(1)}, pred[2,2]{0,1:T(4,128)(4,1)}, u32[]{:S(2)}) copy-start(pred[2,2]{0,1:T(4,128)(4,1)} %get-tuple-element.16) | copy-start | bytes 16
  368.5 6.6 copy-start.9
  368.5 6.7 copy-start.11
  368.5 7.6 copy-start.7
  368.5 7.7 copy-start.10
  368.6 8.1 %copy-start.6 = (f32[2,8]{0,1:T(8,128)S(1)}, f32[2,8]{0,1:T(8,128)}, u32[]{:S(2)}) copy-start(f32[2,8]{0,1:T(8,128)} %get-tuple-element.21) | copy-start | bytes 196
  368.6 8.1 %copy-start.14 = (pred[2,4,1,1]{1,2,3,0:T(4,128)(4,1)S(1)}, pred[2,4,1,1]{1,2,3,0:T(4,128)(4,1)}, u32[]{:S(2)}) copy-start(pred[2,4,1,1]{1,2,3,0:T(4,128)(4,1)} %copy-done.13) | copy-start | bytes 28
  376.7 6.0 copy-start.1
  376.7 6.6 copy-start.5
  382.7 6.1 collective-permute-start.5
  382.7 38.9 %collective-permute-start = (bf16[2,1024,256]{2,1,0:T(8,128)(2,1)S(1)}, bf16[2,1024,256]{2,1,0:T(8,128)(2,1)}, u32[]{:S(2)}, u32[]{:S(2)}) collective-permute-start(bf16[2,1024,256]{2,1,0:T(8,128)(2,1)S(1)} %bitcast.185), channel_id=1, source_target_pairs={{0,1},{1,0},{2,3},{3,2},{4,5},{5,4},{6,7},{7,6},{8,9},{9,8},{10,11... | collective-permute-start | bytes 3145736 | tf_op jit(solution)/shard_map/ppermute | solution.py:62
  383.2 46.0 %collective-permute-start.1 = (bf16[2,1024,256]{2,1,0:T(8,128)(2,1)}, bf16[2,1024,256]{2,1,0:T(8,128)(2,1)}, u32[]{:S(2)}, u32[]{:S(2)}) collective-permute-start(bf16[2,1024,256]{2,1,0:T(8,128)(2,1)} %bitcast.170), channel_id=1, source_target_pairs={{0,1},{1,0},{2,3},{3,2},{4,5},{5,4},{6,7},{7,6},{8,9},{9,8},{10,11... | collective-permute-start | bytes 3145736 | tf_op jit(solution)/shard_map/ppermute | solution.py:63
Sparse Core Ops, SparseCore 0:
  490.8 284.1 reduce-scatter.1
where the time goes:
time: 797 us; the launch traced here: 788 us
  waiting for transfers between devices  285 us (36%)
  matrix products  212 us (27%)
  local copies, waits for them, and re-layouts  182 us (23%)
  other arithmetic  87.2 us (11%)
  between operations  14 us (2%)
    reduce_scatter x1, waiting for transfers between devices, device_fn(): reduced = lax.psum_scatter(part_out, 'tp', scatter_dimension=1, tiled=True)  284 us
    another operation x9, local copies, waits for them, and re-layouts, pick_rows(): split_rows = source.reshape(kept_rows, value_a8, local_heads, head_dim)  62.4 us
    dot_general x4, matrix products, attend(): jnp.einsum('hast,hatd->hasd', weights.astype(jnp.bfloat16), v_sel, prefer...  53.7 us
    dot_general x9, matrix products, pick_rows(): jnp.einsum('sihd,hi->hsd', split_rows, phase_bf, preferred_element_type=j...  51.2 us
    dot_general x4, matrix products, attend(): jnp.einsum('hasd,hatd->hast', q_sel, k_sel, preferred_element_type=jnp.fl...  49.1 us
    dot_general x3, matrix products, project(): jnp.dot(hidden, weight, preferred_element_type=jnp.float32)  42.8 us
    reduce_sum x4, other arithmetic, attend(): row_sum = jnp.sum(weights, axis=-1, keepdims=True)  39.8 us
    reshape x3, local copies, waits for them, and re-layouts, device_fn(): jnp.einsum('hsd,hi->sihd', attn_out.reshape(local_heads, kept_rows, head_...  26.8 us
  transfers between devices with their start and end apart: 9, of which 2 were waited for; matrix products, arithmetic and copies ran while one was open for 48% of the time, Pallas kernels for 0%

commit v1 on v0

v1 whole, which is shorter than its diff:
```python
import functools

import jax
import jax.numpy as jnp
from jax import lax
from jax.experimental import pallas as pl
from jax.experimental.pallas import tpu as pltpu
from jax.sharding import PartitionSpec as P

SEG_BASE = 2048
PHASES = 8
SLOT = (0, 4, 2, 6, 1, 5, 3, 7)
F32 = jnp.float32
BF16 = jnp.bfloat16


def _layer(dims, hidden, wq, wk, wv, wo, bias, out, hbuf, wqkv, pf, qs, ks, vs, k2, v2, k3, v3, wfull, osend, ofull,
           relay, outsend, orelay, h_sem, w_sem, wo_loc, wo_s, wo_r, wof_s, wof_r, wod_s, wod_r, kv2_s, kv2_r, kv3_s,
           kv3_r, o_s, o_r, r_s, r_r, f_s, f_r, u_s, u_r, ur_s, ur_r, uf_s, uf_r, u_loc):
    block_rows, half, dim, scale = dims
    tp_size = 4
    y = lax.axis_index('tp')
    sp = lax.axis_index('sp')
    core = lax.rem(sp, 2)
    up = lax.rem(y + 1, tp_size)
    far = lax.rem(y + 2, tp_size)
    down = lax.rem(y + 3, tp_size)
    tokens = hidden.shape[0]
    num_blocks = tokens // block_rows
    phase_rows = block_rows // PHASES
    quarter = dim // 2
    cols = outsend.shape[-1]

    def sp_peer(dist):
        base = (sp // 4) * 4
        pos = lax.rem(sp, 4)
        if dist == 1:
            other = pos + 1 - 2 * lax.rem(pos, 2)
        elif dist == 2:
            other = lax.rem(pos + 2, 4)
        else:
            other = 3 - pos
        return base + other

    partner = sp_peer(1)

    def remote(src, dst, ssem, rsem, dev):
        return pltpu.make_async_remote_copy(src_ref=src, dst_ref=dst, send_sem=ssem, recv_sem=rsem, device_id=dev,
                                            device_id_type=pl.DeviceIdType.MESH)

    def load_hidden(b):
        slot = lax.rem(b, 3)
        return pltpu.make_async_copy(hidden.at[pl.ds(b * block_rows, block_rows), :], hbuf.at[slot], h_sem.at[slot])

    w_loads = [pltpu.make_async_copy(w, wqkv.at[n], w_sem.at[n]) for n, w in enumerate((wq, wk, wv))]
    load_hidden(0).start()
    w_loads[0].start()
    load_hidden(1).start()
    w_loads[1].start()
    w_loads[2].start()
    wo_local = [pltpu.make_async_copy(wo.at[pl.ds(i * dim, dim), :], wfull.at[y, i], wo_loc.at[i]) for i in range(2)]
    for c in wo_local:
        c.start()

    barrier = pltpu.get_barrier_semaphore()
    peers = [{'tp': up}, {'tp': far}, {'tp': down}] + [{'sp': sp_peer(d)} for d in (1, 2, 3)]
    for dev in peers:
        pl.semaphore_signal(barrier, inc=1, device_id=dev, device_id_type=pl.DeviceIdType.MESH)
    pl.semaphore_wait(barrier, len(peers))

    dirs = (up, down)
    wo_send = [remote(wo.at[pl.ds(core * dim, dim), :], wfull.at[y, core], wo_s.at[n], wo_r.at[n], {'tp': dirs[n]})
               for n in range(2)]
    for c in wo_send:
        c.start()
    near = (down, up)
    wo_part = [pl.ds(0, quarter), pl.ds(quarter, quarter)]
    wo_fwd = [remote(wfull.at[near[n], core, wo_part[n]], wfull.at[near[n], core, wo_part[n]], wof_s.at[n],
                     wof_r.at[n], {'tp': dirs[n]}) for n in range(2)]
    wo_d2d = [remote(wfull.at[near[n], core], wfull.at[near[n], core], wod_s.at[n], wod_r.at[n], {'sp': partner})
              for n in range(2)]
    wo_d2d += [remote(wfull.at[far, core, wo_part[n]], wfull.at[far, core, wo_part[n]], wod_s.at[2 + n],
                      wod_r.at[2 + n], {'sp': partner}) for n in range(2)]

    w_loads[0].wait()
    w_loads[1].wait()
    w_loads[2].wait()

    def project(b, carry):
        load_hidden(b).wait()

        @pl.when(b + 2 < num_blocks)
        def _():
            load_hidden(b + 2).start()

        rows = hbuf[lax.rem(b, 3)]
        s = b // (num_blocks // 2)
        r0 = pl.multiple_of(lax.rem(b, num_blocks // 2) * phase_rows, phase_rows)
        for n, dst in enumerate((qs, ks, vs)):
            for i in range(2):
                res = jnp.dot(rows, wqkv[n, :, i * dim:(i + 1) * dim], preferred_element_type=F32)
                if n == 0:
                    res = res * scale
                for c in range(dim // 128):
                    buf = pf.at[n * 2 + i, c]
                    buf[...] = res[:, c * 128:(c + 1) * 128]
                    for ph in range(PHASES):
                        picked = buf[pl.ds(ph, phase_rows, stride=PHASES), :]
                        dst[i, SLOT[ph], s, pl.ds(r0, phase_rows), c * 128:(c + 1) * 128] = picked.astype(BF16)
        return carry

    lax.fori_loop(0, num_blocks, project, 0)

    u_y = lax.rem(y, 2) * 2 + y // 2
    pair_y = lax.rem(y, 2) * 2
    kv2 = []
    kv3 = []
    for n, (src, two, three) in enumerate(((ks, k2, k3), (vs, v2, v3))):
        for i in range(2):
            kv2.append(remote(src.at[i, pl.ds(4 * i + pair_y, 2)], two.at[i], kv2_s.at[n, i], kv2_r.at[n, i],
                              {'sp': partner}))
            for d in (2, 3, 1):
                kv3.append(remote(src.at[i, 4 * i + u_y], three.at[d - 1, i], kv3_s.at[d - 1, n, i],
                                  kv3_r.at[d - 1, n, i], {'sp': sp_peer(d)}))
    for c in kv2:
        c.start()
    for c in kv3:
        c.start()
    for n in range(2):
        wo_send[n].wait_recv()
        wo_fwd[n].start()
    for n in range(2):
        wo_d2d[n].start()

    def attend(q, keys, values):
        logits = [lax.dot_general(q, k, (((1,), (1,)), ((), ())), preferred_element_type=F32) for k in keys]
        top = logits[0]
        for x in logits[1:]:
            top = jnp.maximum(top, x)
        top = jnp.max(top, axis=1, keepdims=True)
        total = None
        numer = None
        for x, v in zip(logits, values):
            e = jnp.exp(x - top)
            total = e if total is None else total + e
            part = jnp.dot(e.astype(BF16), v, preferred_element_type=F32)
            numer = part if numer is None else numer + part
        return numer, top, jnp.sum(total, axis=1, keepdims=True)

    def head_step(t, s, i, level, dst):
        u = lax.rem(t, 2) * 2 + t // 2
        slot_a = 4 * i + u
        slot_b = 4 * (1 - i) + u
        q_a = qs[i, slot_a, s]
        q_b = qs[i, slot_b, s]
        n0, m0, l0 = attend(jnp.concatenate([q_a, q_b], axis=0), [ks[i, c, s] for c in range(PHASES)],
                            [vs[i, c, s] for c in range(PHASES)])
        dst[1 - i] = (n0[half:] / l0[half:]).astype(BF16)
        parts = [(n0[:half], m0[:half], l0[:half])]
        tiles = [(4 * i + c, h) for c in range(4) for h in range(2)]
        parts.append(attend(q_a, [ks[i, c, h] for c, h in tiles], [vs[i, c, h] for c, h in tiles]))
        if level >= 1:
            tiles = [(c, h) for c in range(2) for h in range(2)]
            base = 4 * i + pair_y
            parts.append(attend(q_a, [ks[i, base + c, h] for c, h in tiles] + [k2[i, c, h] for c, h in tiles],
                                [vs[i, base + c, h] for c, h in tiles] + [v2[i, c, h] for c, h in tiles]))
        if level >= 2:
            mine = 4 * i + u_y
            tiles = [(d, h) for d in range(3) for h in range(2)]
            parts.append(attend(q_a, [ks[i, mine, h] for h in range(2)] + [k3[d, i, h] for d, h in tiles],
                                [vs[i, mine, h] for h in range(2)] + [v3[d, i, h] for d, h in tiles]))
        scores = [m + bias[j, 2 * y + i] for j, (_, m, _) in enumerate(parts)]
        best = functools.reduce(jnp.maximum, scores)
        num = None
        den = None
        for (n, _, l), sc in zip(parts, scores):
            w = jnp.exp(sc - best)
            num = n * w if num is None else num + n * w
            den = l * w if den is None else den + l * w
        dst[i] = (num / den).astype(BF16)

    def o_direct(n, s, i):
        dev = lax.rem(y + 1 + 2 * n, tp_size)
        return remote(osend.at[n, s, i], ofull.at[y, s, i], o_s.at[n, s, i], o_r.at[n, s, i], {'tp': dev})

    def o_relay(s, i):
        dev = lax.rem(y + 1 + 2 * i, tp_size)
        return remote(osend.at[2, s, i], relay.at[s, i], r_s.at[s, i], r_r.at[s, i], {'tp': dev})

    def o_forward(s, i):
        origin = near[i]
        return remote(relay.at[s, i], ofull.at[origin, s, i], f_s.at[s, i], f_r.at[s, i], {'tp': dirs[i]})

    def forward_relay(s):
        for i in range(2):
            o_relay(s, i).wait_recv()
            o_forward(s, i).start()

    def attention_half(s, carry):
        def near_step(j, c):
            n = j // 2
            i = lax.rem(j, 2)
            head_step(lax.rem(y + 1 + 2 * n, tp_size), s, i, 0, osend.at[n, s, i])
            o_direct(n, s, i).start()
            return c

        lax.fori_loop(0, 4, near_step, 0)

        @pl.when(s == 0)
        def _():
            for c in kv2:
                c.wait_recv()

        @pl.when(s == 1)
        def _():
            forward_relay(0)
            for n in range(2):
                wo_fwd[n].wait_recv()
                wo_d2d[2 + n].start()

        def far_step(i, c):
            head_step(far, s, i, 1, osend.at[2, s, i])
            o_relay(s, i).start()
            return c

        lax.fori_loop(0, 2, far_step, 0)

        @pl.when(s == 0)
        def _():
            for c in kv3:
                c.wait_recv()

        def own_step(i, c):
            head_step(y, s, i, 2, ofull.at[y, s, i])
            return c

        lax.fori_loop(0, 2, own_step, 0)
        return carry

    lax.fori_loop(0, 2, attention_half, 0)
    forward_relay(1)

    for c in wo_local:
        c.wait()
    for c in wo_d2d:
        c.wait_recv()

    def out_rows(src, i, s):
        return out.at[2 * src + i, pl.ds(s * half, half), :]

    def u_direct(n, s, i):
        return remote(outsend.at[s, n, i], out_rows(y, i, s), u_s.at[n, s, i], u_r.at[n, s, i], {'tp': dirs[n]})

    def u_relay(s, i):
        return remote(outsend.at[s, 2, i], orelay.at[s, i], ur_s.at[s, i], ur_r.at[s, i], {'tp': dirs[i]})

    def u_forward(s, i):
        return remote(orelay.at[s, i], out_rows(near[i], i, s), uf_s.at[s, i], uf_r.at[s, i], {'tp': dirs[i]})

    def u_own(s, i):
        return pltpu.make_async_copy(outsend.at[s, 3, i], out_rows(y, i, s), u_loc.at[s, i])

    def out_half(s):
        for i in range(2):
            for n in range(2):
                o_direct(n, s, i).wait_recv()
            o_forward(s, i).wait_recv()
        for n, t in ((2, far), (0, up), (1, down), (3, y)):
            c0 = pl.multiple_of(t * cols, cols)
            acc = None
            for src in range(tp_size):
                for i in range(2):
                    lhs = ofull[src, s, i].reshape(2 * half, dim)
                    part = jnp.dot(lhs, wfull[src, i, :, pl.ds(c0, cols)], preferred_element_type=F32)
                    acc = part if acc is None else acc + part
            outsend[s, n] = acc.astype(BF16).reshape(2, half, cols)
            for i in range(2):
                if n == 2:
                    u_relay(s, i).start()
                elif n == 3:
                    u_own(s, i).start()
                else:
                    u_direct(n, s, i).start()

    def forward_out(s):
        for i in range(2):
            u_relay(s, i).wait_recv()
            u_forward(s, i).start()

    out_half(0)
    forward_out(0)
    out_half(1)
    forward_out(1)

    for c in wo_send + wo_fwd + wo_d2d + kv2 + kv3:
        c.wait_send()
    for s in range(2):
        for i in range(2):
            for n in range(2):
                o_direct(n, s, i).wait_send()
                u_direct(n, s, i).wait()
            o_relay(s, i).wait_send()
            o_forward(s, i).wait_send()
            u_relay(s, i).wait_send()
            u_forward(s, i).wait()
            u_own(s, i).wait()


def _natural_order(src, out, buf):
    rows = src.shape[1]
    for c in range(src.shape[2] // 128):
        lanes = slice(c * 128, (c + 1) * 128)
        for ph in range(PHASES):
            buf[c, pl.ds(ph, rows, stride=PHASES), :] = src[ph, :, lanes].astype(F32)
        out[:, lanes] = buf[c].astype(BF16)


def solution(mesh):
    head_groups = mesh.shape['tp']

    def device_fn(hidden, w_query, w_key, w_value, w_out, branch_bias):
        tokens, model_width = hidden.shape
        num_branches, num_heads = branch_bias.shape
        dim = model_width // num_heads
        local_cols = w_query.shape[1]
        cols = model_width // head_groups
        half = tokens // PHASES // 2
        block_rows = min(256, tokens // 4)
        assert head_groups == 4 and num_branches == 4 and num_heads == PHASES and local_cols == 2 * dim
        assert half * PHASES == seg_rows(tokens)
        any_spec = pl.BlockSpec(memory_space=pl.ANY)
        dma = pltpu.SemaphoreType.DMA
        tile = (half, dim)
        vm = lambda *shape: pltpu.VMEM(shape, BF16)
        phase_major = pl.pallas_call(
            functools.partial(_layer, (block_rows, half, dim, dim ** -0.5)),
            out_shape=jax.ShapeDtypeStruct((PHASES, 2 * half, cols), BF16),
            in_specs=[any_spec] * 5 + [pl.BlockSpec(memory_space=pltpu.SMEM)],
            out_specs=any_spec,
            scratch_shapes=[
                vm(3, block_rows, model_width), vm(3, model_width, local_cols),
                pltpu.VMEM((6, dim // 128, block_rows, 128), F32),
                vm(2, PHASES, 2, *tile), vm(2, PHASES, 2, *tile), vm(2, PHASES, 2, *tile),
                vm(2, 2, 2, *tile), vm(2, 2, 2, *tile), vm(3, 2, 2, *tile), vm(3, 2, 2, *tile),
                vm(4, 2, dim, model_width),
                vm(3, 2, 2, 2, *tile), vm(4, 2, 2, 2, *tile), vm(2, 2, 2, *tile),
                vm(2, 4, 2, half, cols), vm(2, 2, half, cols),
                dma((3,)), dma((3,)), dma((2,)),
                dma((2,)), dma((2,)), dma((2,)), dma((2,)), dma((4,)), dma((4,)),
                dma((2, 2)), dma((2, 2)), dma((3, 2, 2)), dma((3, 2, 2)),
                dma((2, 2, 2)), dma((2, 2, 2)), dma((2, 2)), dma((2, 2)), dma((2, 2)), dma((2, 2)),
                dma((2, 2, 2)), dma((2, 2, 2)), dma((2, 2)), dma((2, 2)), dma((2, 2)), dma((2, 2)), dma((2, 2)),
            ],
            compiler_params=pltpu.CompilerParams(collective_id=0, has_side_effects=True,
                                                 vmem_limit_bytes=67043328),
            name='layer',
        )(hidden, w_query, w_key, w_value, w_out, branch_bias)
        rows = min(64, half)
        return pl.pallas_call(
            _natural_order,
            grid=(2 * half // rows,),
            in_specs=[pl.BlockSpec((PHASES, rows, cols), lambda b: (0, b, 0))],
            out_specs=pl.BlockSpec((PHASES * rows, cols), lambda b: (b, 0)),
            out_shape=jax.ShapeDtypeStruct((tokens, cols), BF16),
            scratch_shapes=[pltpu.VMEM((cols // 128, PHASES * rows, 128), F32)],
            name='natural_order',
        )(phase_major)

    return jax.shard_map(device_fn, mesh=mesh, in_specs=(P(('dp', 'sp'), None), P(None, 'tp'), P(None, 'tp'), P(None, 'tp'), P('tp', None), P(None, None)), out_specs=P(('dp', 'sp'), 'tp'), check_vma=False)


def seg_rows(tokens):
    return SEG_BASE if tokens >= 2 * SEG_BASE else tokens // 2
```

time: 797 us -> 188 us (0.24); the launches traced: 788 us -> 188 us
  waiting for transfers between devices: 285 us -> 0 us
  matrix products: 212 us -> 0 us
  Pallas kernels: 0 us -> 188 us
  local copies, waits for them, and re-layouts: 182 us -> 0 us
  other arithmetic: 87.2 us -> 0 us
  between operations: 14 us -> 0.01 us
    reduce_scatter x1 -> x0, waiting for transfers between devices: 284 us -> none  [device_fn(): reduced = lax.psum_scatter(part_out, 'tp', scatter_dimension=1, tiled=True)]
    dot_general x21 -> x0, matrix products: 212 us -> none  [the longest x4 53.7 us: attend(): jnp.einsum('hast,hatd->hasd', weights.astype(jnp.bfloat16), v_sel, prefer...]
    pallas_call x0 -> x2, Pallas kernels: none -> 188 us  [the longest x1 180 us: device_fn(): pl.pallas_call(functools.partial(_layer, (block_rows, half, dim, dim ** (...]
    another operation x12 -> x0, local copies, waits for them, and re-layouts: 62.7 us -> none  [the longest x9 62.4 us: pick_rows(): split_rows = source.reshape(kept_rows, value_a8, local_heads, head_dim)]
    reduce_sum x4 -> x0, other arithmetic: 39.8 us -> none  [attend(): row_sum = jnp.sum(weights, axis=-1, keepdims=True)]
    convert_element_type x6 -> x0, local copies, waits for them, and re-layouts: 38.4 us -> none  [the longest x3 19.4 us: project(): jnp.dot(hidden, weight, preferred_element_type=jnp.float32)]
    reshape x9 -> x0, local copies, waits for them, and re-layouts: 34.3 us -> none  [the longest x3 26.8 us: device_fn(): jnp.einsum('hsd,hi->sihd', attn_out.reshape(local_heads, kept_rows, head_...]
    unnamed x33 -> x0, local copies, waits for them, and re-layouts: 19.4 us -> none
  transfers between devices with their start and end apart: 9 -> 0, of which waited for: 2 -> 0; matrix products, arithmetic and copies ran while one was open for 48% -> 0% of each run, Pallas kernels for 0% -> 0%
where the time goes in v1:
time: 188 us
  Pallas kernels  188 us (100%)
    pallas_call x1, Pallas kernels, device_fn(): pl.pallas_call(functools.partial(_layer, (block_rows, half, dim, dim ** (...  180 us
    pallas_call x1, Pallas kernels, device_fn(): pl.pallas_call(_natural_order, grid=(2 * half // rows,), in_specs=[pl.Blo...  7.52 us

profile of v1, /device:TPU:97, one launch (start us, length us, event | category | flops | bytes accessed | tf_op | source)
XLA Modules:
  0.0 187.6 jit_solution(11483013186545141504)
XLA Ops:
  0.0 180.0 %layer.1.src = bf16[8,512,512]{2,1,0:T(8,128)(2,1)} custom-call(bf16[4096,2048]{1,0:T(8,128)(2,1)} %hidden.1, bf16[2048,512]{1,0:T(8,128)(2,1)} %wq.1, bf16[2048,512]{1,0:T(8,128)(2,1)} %wk.1, bf16[2048,512]{1,0:T(8,128)(2,1)} %wv.1, bf16[512,2048]{1,0:T(8,128)(2,1)} %wo.1, f32[4,8]{1,0:T(4,128)} %bias.1), custom_call_target="tpu_custom_call" | custom-call | tf_op jit(solution)/shard_map/layer/pallas_call | solution.py:335
  180.0 7.5 %natural_order.1 = bf16[4096,512]{1,0:T(8,128)(2,1)} custom-call(bf16[8,512,512]{2,1,0:T(8,128)(2,1)} %layer.1.src), custom_call_target="tpu_custom_call" | custom-call | tf_op jit(solution)/shard_map/natural_order/pallas_call | solution.py:359

commit v2 on v1

v2 whole, which is shorter than its diff:
```python
import functools

import jax
import jax.numpy as jnp
from jax import lax
from jax.experimental import pallas as pl
from jax.experimental.pallas import tpu as pltpu
from jax.sharding import PartitionSpec as P

SEG_BASE = 2048
PHASES = 8
SLOT = (0, 4, 2, 6, 1, 5, 3, 7)
F32 = jnp.float32
BF16 = jnp.bfloat16


def _layer(dims, hidden, wq, wk, wv, wo, bias, out, hbuf, wqkv, pf, qs, ks, vs, k2, v2, k3, v3, wfull, osend, ofull,
           relay_a, relay_b, orelay, h_sem, w_sem, wo_loc, wy_s, wy_r, wyf_s, wyf_r, wx_s, wx_r, wxf_s, wxf_r,
           wd_s, wd_r, wdf_s, wdf_r, kv2_s, kv2_r, kv3_s, kv3_r, oa_s, oa_r, ra_s, ra_r, fa_s, fa_r, ob_s, ob_r, rb_s,
           rb_r, fb_s, fb_r, u_s, u_r, ur_s, ur_r, uf_s, uf_r, u_loc):
    block_rows, half, dim, scale = dims
    tp_size = 4
    y = lax.axis_index('tp')
    sp = lax.axis_index('sp')
    up = lax.rem(y + 1, tp_size)
    far = lax.rem(y + 2, tp_size)
    down = lax.rem(y + 3, tp_size)
    tokens = hidden.shape[0]
    num_blocks = tokens // block_rows
    half_blocks = num_blocks // 2
    phase_rows = block_rows // PHASES
    slices, _, piece, _ = wfull.shape
    cols = orelay.shape[-1]

    def sp_peer(dist):
        base = (sp // 4) * 4
        pos = lax.rem(sp, 4)
        if dist == 1:
            other = pos + 1 - 2 * lax.rem(pos, 2)
        elif dist == 2:
            other = lax.rem(pos + 2, 4)
        else:
            other = 3 - pos
        return base + other

    partner = sp_peer(1)
    right = lax.rem(sp + 2, slices)
    opposite = lax.rem(sp + slices // 2, slices)
    left = lax.rem(sp + slices - 2, slices)

    def remote(src, dst, ssem, rsem, dev):
        return pltpu.make_async_remote_copy(src_ref=src, dst_ref=dst, send_sem=ssem, recv_sem=rsem, device_id=dev,
                                            device_id_type=pl.DeviceIdType.MESH)

    def load_hidden(b):
        slot = lax.rem(b, 2)
        return pltpu.make_async_copy(hidden.at[pl.ds(b * block_rows, block_rows), :], hbuf.at[slot], h_sem.at[slot])

    w_loads = [pltpu.make_async_copy(w, wqkv.at[n], w_sem.at[n]) for n, w in enumerate((wq, wk, wv))]
    load_hidden(0).start()
    w_loads[0].start()
    w_loads[1].start()
    w_loads[2].start()
    wo_local = [pltpu.make_async_copy(wo.at[pl.ds(j * piece, piece), :], wfull.at[j, y], wo_loc.at[j])
                for j in range(slices)]
    barrier = pltpu.get_barrier_semaphore()
    peers = [{'tp': up}, {'tp': far}, {'tp': down}, {'sp': partner}, {'sp': right}, {'sp': left}]
    for dev in peers:
        pl.semaphore_signal(barrier, inc=1, device_id=dev, device_id_type=pl.DeviceIdType.MESH)

    dirs = (up, down)
    near = (down, up)
    xdirs = (right, left)
    xnear = (left, right)
    part = [pl.ds(0, piece // 2), pl.ds(piece // 2, piece // 2)]
    wo_y = [remote(wo.at[pl.ds(pl.multiple_of(sp * piece, piece), piece), :], wfull.at[sp, y], wy_s.at[n], wy_r.at[n],
                   {'tp': dirs[n]}) for n in range(2)]
    wo_yf = [remote(wfull.at[sp, near[n], part[n]], wfull.at[sp, near[n], part[n]], wyf_s.at[n], wyf_r.at[n],
                    {'tp': dirs[n]}) for n in range(2)]
    others = (up, far, down)

    def wo_x(n, k):
        ref = wfull.at[sp, others[k]]
        return remote(ref, ref, wx_s.at[n, k], wx_r.at[n, k], {'sp': xdirs[n]})

    def wo_xf(n, k):
        ref = wfull.at[xnear[n], others[k], part[n]]
        return remote(ref, ref, wxf_s.at[n, k], wxf_r.at[n, k], {'sp': xdirs[n]})

    def wo_d(j, k):
        ref = wfull.at[(sp, left, right)[j], others[k]]
        return remote(ref, ref, wd_s.at[j, k], wd_r.at[j, k], {'sp': partner})

    def wo_df(n, k):
        ref = wfull.at[opposite, others[k], part[n]]
        return remote(ref, ref, wdf_s.at[n, k], wdf_r.at[n, k], {'sp': partner})

    u_y = lax.rem(y, 2) * 2 + y // 2
    pair_y = lax.rem(y, 2) * 2
    kv = ((ks, k2, k3), (vs, v2, v3))

    def kv2(n, i):
        src, two, _ = kv[n]
        return remote(src.at[i, pl.ds(4 * i + pair_y, 2)], two.at[i], kv2_s.at[n, i], kv2_r.at[n, i], {'sp': partner})

    def kv3(d, n, i):
        src, _, three = kv[n]
        ref = three.at[1, i] if d == 3 else src.at[i, 4 * i + u_y]
        return remote(ref, three.at[d - 1, i], kv3_s.at[d - 1, n, i], kv3_r.at[d - 1, n, i],
                      {'sp': partner if d == 3 else sp_peer(d)})

    def attend(q, keys, values):
        logits = [lax.dot_general(q, k, (((1,), (1,)), ((), ())), preferred_element_type=F32) for k in keys]
        top = logits[0]
        for x in logits[1:]:
            top = jnp.maximum(top, x)
        top = jnp.max(top, axis=1, keepdims=True)
        total = None
        numer = None
        for x, v in zip(logits, values):
            e = jnp.exp(x - top)
            total = e if total is None else total + e
            piece_sum = jnp.dot(e.astype(BF16), v, preferred_element_type=F32)
            numer = piece_sum if numer is None else numer + piece_sum
        return numer, top, jnp.sum(total, axis=1, keepdims=True)

    def slot_of(t):
        return lax.rem(t, 2) * 2 + t // 2

    def step_b(s, i, t0, t1, dst0, dst1):
        q = jnp.concatenate([qs[i, 4 * (1 - i) + slot_of(t0), s], qs[i, 4 * (1 - i) + slot_of(t1), s]], axis=0)
        n, _, l = attend(q, [ks[i, c, s] for c in range(PHASES)], [vs[i, c, s] for c in range(PHASES)])
        o = (n / l).astype(BF16)
        dst0[...] = o[:half]
        dst1[...] = o[half:]

    def step_a(t, i, level, dst, s=None):
        slot = 4 * i + slot_of(t)
        zero = [attend(qs[i, slot, h], [ks[i, c, h] for c in range(PHASES)], [vs[i, c, h] for c in range(PHASES)])
                for h in (range(2) if s is None else (s,))]
        if s is None:
            parts = [tuple(jnp.concatenate([a, b], axis=0) for a, b in zip(*zero))]
            q = qs[i, slot].reshape(2 * half, dim)
        else:
            parts = zero
            q = qs[i, slot, s]
        tiles = [(4 * i + c, h) for c in range(4) for h in range(2)]
        parts.append(attend(q, [ks[i, c, h] for c, h in tiles], [vs[i, c, h] for c, h in tiles]))
        if level >= 1:
            tiles = [(c, h) for c in range(2) for h in range(2)]
            base = 4 * i + pair_y
            parts.append(attend(q, [ks[i, base + c, h] for c, h in tiles] + [k2[i, c, h] for c, h in tiles],
                                [vs[i, base + c, h] for c, h in tiles] + [v2[i, c, h] for c, h in tiles]))
        if level >= 2:
            mine = 4 * i + u_y
            tiles = [(d, h) for d in range(3) for h in range(2)]
            parts.append(attend(q, [ks[i, mine, h] for h in range(2)] + [k3[d, i, h] for d, h in tiles],
                                [vs[i, mine, h] for h in range(2)] + [v3[d, i, h] for d, h in tiles]))
        scores = [m + bias[j, 2 * y + i] for j, (_, m, _) in enumerate(parts)]
        best = functools.reduce(jnp.maximum, scores)
        num = None
        den = None
        for (n, _, l), sc in zip(parts, scores):
            w = jnp.exp(sc - best)
            num = n * w if num is None else num + n * w
            den = l * w if den is None else den + l * w
        dst[...] = (num / den).astype(BF16).reshape(dst.shape)

    def along(n):
        return {'tp': lax.rem(y + 1 + 2 * n, tp_size)}

    def a_direct(n, i):
        return remote(osend.at[n, i, i], ofull.at[y, i, i], oa_s.at[n, i], oa_r.at[n, i], along(n))

    def a_relay(i):
        return remote(osend.at[2, i, i], relay_a.at[i], ra_s.at[i], ra_r.at[i], along(i))

    def origin(n):
        return lax.rem(y + 3 - 2 * n, tp_size)

    def a_forward(i):
        return remote(relay_a.at[i], ofull.at[origin(i), i, i], fa_s.at[i], fa_r.at[i], along(i))

    def b_direct(n, s, i):
        return remote(osend.at[n, i, 1 - i, s], ofull.at[y, i, 1 - i, s], ob_s.at[n, s, i], ob_r.at[n, s, i], along(n))

    def b_relay(s, i):
        return remote(osend.at[2, i, 1 - i, s], relay_b.at[s, i], rb_s.at[s, i], rb_r.at[s, i], along(i))

    def b_forward(s, i):
        return remote(relay_b.at[s, i], ofull.at[origin(i), i, 1 - i, s], fb_s.at[s, i], fb_r.at[s, i], along(i))

    def forward_b(s):
        for i in range(2):
            b_relay(s, i).wait_recv()
            b_forward(s, i).start()

    for c in w_loads:
        c.wait()

    def first(s, carry):
        def project(r, c):
            b = s * half_blocks + r
            load_hidden(b).wait()

            @pl.when(b + 1 < num_blocks)
            def _():
                load_hidden(b + 1).start()

            @pl.when(b == 1)
            def _():
                pl.semaphore_wait(barrier, len(peers))
                for c in wo_y + wo_local:
                    c.start()

            @pl.when(b == half_blocks - 2)
            def _():
                for n in range(2):
                    wo_y[n].wait_recv()
                    wo_yf[n].start()

            @pl.when(b == half_blocks + 1)
            def _():
                for c in wo_yf:
                    c.wait_recv()
                for k in range(3):
                    for n in range(2):
                        wo_x(n, k).start()
                    wo_d(0, k).start()

            @pl.when(b == num_blocks - 2)
            def _():
                forward_b(0)

            rows = hbuf[lax.rem(b, 2)]
            r0 = pl.multiple_of(r * phase_rows, phase_rows)
            for n, dst in enumerate((qs, ks, vs)):
                for i in range(2):
                    res = jnp.dot(rows, wqkv[n, :, i * dim:(i + 1) * dim], preferred_element_type=F32)
                    if n == 0:
                        res = res * scale
                    for g in range(dim // 128):
                        buf = pf.at[n * 2 + i, g]
                        buf[...] = res[:, g * 128:(g + 1) * 128]
                        for ph in range(PHASES):
                            picked = buf[pl.ds(ph, phase_rows, stride=PHASES), :]
                            dst[i, SLOT[ph], s, pl.ds(r0, phase_rows), g * 128:(g + 1) * 128] = picked.astype(BF16)
            return c

        lax.fori_loop(0, half_blocks, project, 0)

        @pl.when(s == 1)
        def _():
            for i in range(2):
                for n in range(2):
                    kv2(n, i).start()
                    for d in (2, 1):
                        kv3(d, n, i).start()

        def b_pair(i, c):
            step_b(s, i, far, y, osend.at[2, i, 1 - i, s], ofull.at[y, i, 1 - i, s])
            step_b(s, i, up, down, osend.at[0, i, 1 - i, s], osend.at[1, i, 1 - i, s])
            b_relay(s, i).start()
            for n in range(2):
                b_direct(n, s, i).start()
            return c

        lax.fori_loop(0, 2, b_pair, 0)
        return carry

    lax.fori_loop(0, 2, first, 0)

    def outsend(n, i, rows=slice(0, 2 * half)):
        k = 2 * n + i
        per = wqkv.shape[1] // (2 * half)
        return wqkv.at[k // per, pl.ds(pl.multiple_of(lax.rem(k, per) * 2 * half, 2 * half) + rows.start, rows.stop - rows.start), :]

    def u_direct(n, i):
        return remote(outsend(n, i), out.at[2 * y + i], u_s.at[n, i], u_r.at[n, i], {'tp': dirs[n]})

    def u_relay(i, n):
        return remote(outsend(2, i, slice(n * half, (n + 1) * half)), orelay.at[i, n], ur_s.at[i, n], ur_r.at[i, n],
                      {'tp': dirs[n]})

    def u_forward(i, n):
        return remote(orelay.at[i, n], out.at[2 * near[n] + i, pl.ds(n * half, half)], uf_s.at[i, n], uf_r.at[i, n],
                      {'tp': dirs[n]})

    def forward_u(i):
        for n in range(2):
            u_relay(i, n).wait_recv()
            u_forward(i, n).start()

    def u_own(i):
        return pltpu.make_async_copy(outsend(3, i), out.at[2 * y + i], u_loc.at[i])

    for k in range(3):
        for n in range(2):
            wo_x(n, k).wait_recv()
            wo_xf(n, k).start()
            wo_d(1 + n, k).start()

    def others_first(i, carry):
        for n in range(2):
            kv2(n, i).wait_recv()
        step_a(far, i, 1, osend.at[2, i, i])
        a_relay(i).start()

        @pl.when(i == 0)
        def _():
            forward_b(1)

        def one(n, c):
            step_a(lax.rem(y + 1 + 2 * n, tp_size), i, 0, osend.at[n, i, i])
            a_direct(n, i).start()
            return c

        lax.fori_loop(0, 2, one, 0)
        for m in range(2):
            kv3(2, m, i).wait_recv()
            kv3(3, m, i).start()
        a_relay(i).wait_recv()
        a_forward(i).start()
        return carry

    lax.fori_loop(0, 2, others_first, 0)
    for k in range(3):
        for n in range(2):
            wo_xf(n, k).wait_recv()
            wo_df(n, k).start()

    def own_last(i, carry):
        for m in range(2):
            kv3(1, m, i).wait_recv()
            kv3(3, m, i).wait_recv()

        def own(s, c):
            step_a(y, i, 2, ofull.at[y, i, i, s], s)
            return c

        lax.fori_loop(0, 2, own, 0)

        @pl.when(i == 0)
        def _():
            for c in wo_local:
                c.wait()
            for k in range(3):
                for j in range(3):
                    wo_d(j, k).wait_recv()
                for n in range(2):
                    wo_df(n, k).wait_recv()

        @pl.when(i == 1)
        def _():
            forward_u(0)

        for n in range(2):
            a_direct(n, i).wait_recv()
        a_forward(i).wait_recv()
        for s in range(2):
            for n in range(2):
                b_direct(n, s, 1 - i).wait_recv()
            b_forward(s, 1 - i).wait_recv()
        for n, t in ((2, far), (0, up), (1, down), (3, y)):
            c0 = pl.multiple_of(t * cols, cols)
            acc = None
            for src in range(tp_size):
                for h in range(2):
                    lhs = ofull[src, h, i].reshape(2 * half, dim)
                    eighth = slices // 2
                    rhs = wfull[h * eighth:(h + 1) * eighth, src, :, pl.ds(c0, cols)].reshape(dim, cols)
                    res = jnp.dot(lhs, rhs, preferred_element_type=F32)
                    acc = res if acc is None else acc + res
            outsend(n, i)[...] = acc.astype(BF16)
            if n == 2:
                for r in range(2):
                    u_relay(i, r).start()
            elif n == 3:
                u_own(i).start()
            else:
                u_direct(n, i).start()
        return carry

    lax.fori_loop(0, 2, own_last, 0)
    forward_u(1)

    for c in wo_y + wo_yf:
        c.wait_send()
    for k in range(3):
        for n in range(2):
            wo_x(n, k).wait_send()
            wo_xf(n, k).wait_send()
            wo_df(n, k).wait_send()
        for j in range(3):
            wo_d(j, k).wait_send()
    for i in range(2):
        for n in range(2):
            kv2(n, i).wait_send()
            for d in (1, 2, 3):
                kv3(d, n, i).wait_send()
            a_direct(n, i).wait_send()
            for s in range(2):
                b_direct(n, s, i).wait_send()
            u_direct(n, i).wait()
            u_relay(i, n).wait_send()
            u_forward(i, n).wait()
        a_relay(i).wait_send()
        a_forward(i).wait_send()
        for s in range(2):
            b_relay(s, i).wait_send()
            b_forward(s, i).wait_send()
        u_own(i).wait()


def _natural_order(src, out):
    cols = src.shape[2]
    group = min(32, src.shape[1])
    size = group * PHASES
    to = lax.broadcasted_iota(jnp.int32, (size, size), 0)
    frm = lax.broadcasted_iota(jnp.int32, (size, size), 1)
    perm = jnp.where(frm == lax.rem(to, PHASES) * group + to // PHASES, 1.0, 0.0).astype(BF16)
    for g in range(src.shape[1] // group):
        rows = src[:, g * group:(g + 1) * group, :].reshape(size, cols)
        out[g * size:(g + 1) * size, :] = jnp.dot(perm, rows, preferred_element_type=F32).astype(BF16)


def solution(mesh):
    head_groups = mesh.shape['tp']
    seq_size = mesh.shape['sp']

    def device_fn(hidden, w_query, w_key, w_value, w_out, branch_bias):
        tokens, model_width = hidden.shape
        num_branches, num_heads = branch_bias.shape
        dim = model_width // num_heads
        local_cols = w_query.shape[1]
        cols = model_width // head_groups
        half = tokens // PHASES // 2
        block_rows = min(256, tokens // 16)
        assert head_groups == 4 and num_branches == 4 and num_heads == PHASES and local_cols == 2 * dim
        assert half * PHASES == seg_rows(tokens) and local_cols == cols
        assert 3 * model_width >= 8 * 2 * half and model_width % (2 * half) == 0
        any_spec = pl.BlockSpec(memory_space=pl.ANY)
        dma = pltpu.SemaphoreType.DMA
        tile = (half, dim)
        vm = lambda *shape: pltpu.VMEM(shape, BF16)
        phase_major = pl.pallas_call(
            functools.partial(_layer, (block_rows, half, dim, dim ** -0.5)),
            out_shape=jax.ShapeDtypeStruct((PHASES, 2 * half, cols), BF16),
            in_specs=[any_spec] * 5 + [pl.BlockSpec(memory_space=pltpu.SMEM)],
            out_specs=any_spec,
            scratch_shapes=[
                vm(2, block_rows, model_width), vm(3, model_width, local_cols),
                pltpu.VMEM((6, dim // 128, block_rows, 128), F32),
                vm(2, PHASES, 2, *tile), vm(2, PHASES, 2, *tile), vm(2, PHASES, 2, *tile),
                vm(2, 2, 2, *tile), vm(2, 2, 2, *tile), vm(3, 2, 2, *tile), vm(3, 2, 2, *tile),
                vm(seq_size, head_groups, local_cols // seq_size, model_width),
                vm(3, 2, 2, 2, *tile), vm(4, 2, 2, 2, *tile), vm(2, 2, *tile), vm(2, 2, *tile),
                vm(2, 2, half, cols),
                dma((2,)), dma((3,)), dma((seq_size,)),
                dma((2,)), dma((2,)), dma((2,)), dma((2,)), dma((2, 3)), dma((2, 3)), dma((2, 3)), dma((2, 3)),
                dma((3, 3)), dma((3, 3)), dma((2, 3)), dma((2, 3)),
                dma((2, 2)), dma((2, 2)), dma((3, 2, 2)), dma((3, 2, 2)),
                dma((2, 2)), dma((2, 2)), dma((2,)), dma((2,)), dma((2,)), dma((2,)),
                dma((2, 2, 2)), dma((2, 2, 2)), dma((2, 2)), dma((2, 2)), dma((2, 2)), dma((2, 2)),
                dma((2, 2)), dma((2, 2)), dma((2, 2)), dma((2, 2)), dma((2, 2)), dma((2, 2)), dma((2,)),
            ],
            compiler_params=pltpu.CompilerParams(collective_id=0, has_side_effects=True,
                                                 vmem_limit_bytes=67043328),
            name='layer',
        )(hidden, w_query, w_key, w_value, w_out, branch_bias)
        rows = min(128, half)
        return pl.pallas_call(
            _natural_order,
            grid=(2 * half // rows,),
            in_specs=[pl.BlockSpec((PHASES, rows, cols), lambda b: (0, b, 0))],
            out_specs=pl.BlockSpec((PHASES * rows, cols), lambda b: (b, 0)),
            out_shape=jax.ShapeDtypeStruct((tokens, cols), BF16),
            name='natural_order',
        )(phase_major)

    return jax.shard_map(device_fn, mesh=mesh, in_specs=(P(('dp', 'sp'), None), P(None, 'tp'), P(None, 'tp'), P(None, 'tp'), P('tp', None), P(None, None)), out_specs=P(('dp', 'sp'), 'tp'), check_vma=False)


def seg_rows(tokens):
    return SEG_BASE if tokens >= 2 * SEG_BASE else tokens // 2
```

time: 188 us -> 146 us (0.78)
  Pallas kernels: 188 us -> 146 us
    pallas_call x1, Pallas kernels: 180 us -> 140 us  [device_fn(): pl.pallas_call(functools.partial(_layer, (block_rows, half, dim, dim ** (...]
    pallas_call x1, Pallas kernels: 7.52 us -> 5.54 us  [device_fn(): pl.pallas_call(_natural_order, grid=(2 * half // rows,), in_specs=[pl.Blo...]
where the time goes in v2:
time: 146 us
  Pallas kernels  146 us (100%)
    pallas_call x1, Pallas kernels, device_fn(): pl.pallas_call(functools.partial(_layer, (block_rows, half, dim, dim ** (...  140 us
    pallas_call x1, Pallas kernels, device_fn(): pl.pallas_call(_natural_order, grid=(2 * half // rows,), in_specs=[pl.Blo...  5.54 us

profile of v2, /device:TPU:97, one launch (start us, length us, event | category | flops | bytes accessed | tf_op | source)
XLA Modules:
  0.0 145.7 jit_solution(359220212813541388)
XLA Ops:
  0.0 140.1 %layer.1.src = bf16[8,512,512]{2,1,0:T(8,128)(2,1)} custom-call(bf16[4096,2048]{1,0:T(8,128)(2,1)} %hidden.1, bf16[2048,512]{1,0:T(8,128)(2,1)} %wq.1, bf16[2048,512]{1,0:T(8,128)(2,1)} %wk.1, bf16[2048,512]{1,0:T(8,128)(2,1)} %wv.1, bf16[512,2048]{1,0:T(8,128)(2,1)} %wo.1, f32[4,8]{1,0:T(4,128)} %bias.1), custom_call_target="tpu_custom_call" | custom-call | tf_op jit(solution)/shard_map/layer/pallas_call | solution.py:446
  140.1 5.5 %natural_order.1 = bf16[4096,512]{1,0:T(8,128)(2,1)} custom-call(bf16[8,512,512]{2,1,0:T(8,128)(2,1)} %layer.1.src), custom_call_target="tpu_custom_call" | custom-call | tf_op jit(solution)/shard_map/natural_order/pallas_call | solution.py:472

commit v3 on v2

--- a/solution.py
+++ b/solution.py
@@ -14,10 +14,9 @@
 BF16 = jnp.bfloat16
 
 
-def _layer(dims, hidden, wq, wk, wv, wo, bias, out, hbuf, wqkv, pf, qs, ks, vs, k2, v2, k3, v3, wfull, osend, ofull,
-           relay_a, relay_b, orelay, h_sem, w_sem, wo_loc, wy_s, wy_r, wyf_s, wyf_r, wx_s, wx_r, wxf_s, wxf_r,
-           wd_s, wd_r, wdf_s, wdf_r, kv2_s, kv2_r, kv3_s, kv3_r, oa_s, oa_r, ra_s, ra_r, fa_s, fa_r, ob_s, ob_r, rb_s,
-           rb_r, fb_s, fb_r, u_s, u_r, ur_s, ur_r, uf_s, uf_r, u_loc):
+def _layer(dims, hidden, wq, wk, wv, wo, bias, out, hbuf, wqkv, pf, qs, ks, vs, k2, v2, k3, v3, wfull, obuf, h_sem, w_sem, wo_loc, wy_s, wy_r, wyf_s, wyf_r, wx_s, wx_r, wxf_s, wxf_r,
+           wd_s, wd_r, wdf_s, wdf_r, kv2_s, kv2_r, kv3_s, kv3_r, a_s, a_r, af_s, af_r, b_s, b_r, bf_s, bf_r, u_s, u_r,
+           u_loc):
     block_rows, half, dim, scale = dims
     tp_size = 4
     y = lax.axis_index('tp')
@@ -30,7 +29,7 @@
     half_blocks = num_blocks // 2
     phase_rows = block_rows // PHASES
     slices, _, piece, _ = wfull.shape
-    cols = orelay.shape[-1]
+    cols = wqkv.shape[2]
 
     def sp_peer(dist):
         base = (sp // 4) * 4
@@ -109,7 +108,9 @@
         return remote(ref, three.at[d - 1, i], kv3_s.at[d - 1, n, i], kv3_r.at[d - 1, n, i],
                       {'sp': partner if d == 3 else sp_peer(d)})
 
-    def attend(q, keys, values):
+    def attend(q, keys, values, after=None):
+        if after is not None:
+            q = q + jnp.minimum(after, 0.0).astype(BF16)
         logits = [lax.dot_general(q, k, (((1,), (1,)), ((), ())), preferred_element_type=F32) for k in keys]
         top = logits[0]
         for x in logits[1:]:
@@ -127,12 +128,13 @@
     def slot_of(t):
         return lax.rem(t, 2) * 2 + t // 2
 
-    def step_b(s, i, t0, t1, dst0, dst1):
+    def step_b(s, i, t0, t1, dst0, dst1, after=None):
         q = jnp.concatenate([qs[i, 4 * (1 - i) + slot_of(t0), s], qs[i, 4 * (1 - i) + slot_of(t1), s]], axis=0)
-        n, _, l = attend(q, [ks[i, c, s] for c in range(PHASES)], [vs[i, c, s] for c in range(PHASES)])
+        n, _, l = attend(q, [ks[i, c, s] for c in range(PHASES)], [vs[i, c, s] for c in range(PHASES)], after)
         o = (n / l).astype(BF16)
         dst0[...] = o[:half]
         dst1[...] = o[half:]
+        return l
 
     def step_a(t, i, level, dst, s=None):
         slot = 4 * i + slot_of(t)
@@ -166,37 +168,55 @@
             den = l * w if den is None else den + l * w
         dst[...] = (num / den).astype(BF16).reshape(dst.shape)
 
-    def along(n):
-        return {'tp': lax.rem(y + 1 + 2 * n, tp_size)}
-
-    def a_direct(n, i):
-        return remote(osend.at[n, i, i], ofull.at[y, i, i], oa_s.at[n, i], oa_r.at[n, i], along(n))
-
-    def a_relay(i):
-        return remote(osend.at[2, i, i], relay_a.at[i], ra_s.at[i], ra_r.at[i], along(i))
-
-    def origin(n):
-        return lax.rem(y + 3 - 2 * n, tp_size)
-
-    def a_forward(i):
-        return remote(relay_a.at[i], ofull.at[origin(i), i, i], fa_s.at[i], fa_r.at[i], along(i))
-
-    def b_direct(n, s, i):
-        return remote(osend.at[n, i, 1 - i, s], ofull.at[y, i, 1 - i, s], ob_s.at[n, s, i], ob_r.at[n, s, i], along(n))
-
-    def b_relay(s, i):
-        return remote(osend.at[2, i, 1 - i, s], relay_b.at[s, i], rb_s.at[s, i], rb_r.at[s, i], along(i))
-
-    def b_forward(s, i):
-        return remote(relay_b.at[s, i], ofull.at[origin(i), i, 1 - i, s], fb_s.at[s, i], fb_r.at[s, i], along(i))
+    def flow(f):
+        return ((8, y, up), (9, 4 + y, down), (4 + y, y, down), (y, 4 + y, up))[f]
+
+    def send_a(f, i):
+        here, there, dev = flow(f)
+        return remote(obuf.at[here, i, i], obuf.at[there, i, i], a_s.at[f, i], a_r.at[f, i], {'tp': dev})
+
+    def send_b(f, s, i):
+        here, there, dev = flow(f)
+        return remote(obuf.at[here, i, 1 - i, s], obuf.at[there, i, 1 - i, s], b_s.at[f, s, i], b_r.at[f, s, i],
+                      {'tp': dev})
+
+    def onward(n):
+        return ((down, 4 + down, up), (4 + up, up, down))[n]
+
+    def pass_a(n, i):
+        here, there, dev = onward(n)
+        return remote(obuf.at[here, i, i], obuf.at[there, i, i], af_s.at[n, i], af_r.at[n, i], {'tp': dev})
+
+    def pass_b(n, s, i):
+        here, there, dev = onward(n)
+        return remote(obuf.at[here, i, 1 - i, s], obuf.at[there, i, 1 - i, s], bf_s.at[n, s, i], bf_r.at[n, s, i],
+                      {'tp': dev})
+
+    def forward_a(i):
+        for n in range(2):
+            send_a(n, i).wait_recv()
+            pass_a(n, i).start()
 
     def forward_b(s):
         for i in range(2):
-            b_relay(s, i).wait_recv()
-            b_forward(s, i).start()
+            for n in range(2):
+                send_b(n, s, i).wait_recv()
+                pass_b(n, s, i).start()
 
     for c in w_loads:
         c.wait()
+
+    def place(buf, n, i, b):
+        r0 = pl.multiple_of(lax.rem(b, half_blocks) * phase_rows, phase_rows)
+        for g in range(dim // 128):
+            for ph in range(PHASES):
+                picked = buf[g, pl.ds(ph, phase_rows, stride=PHASES), :]
+                kv_q[n][i, SLOT[ph], b // half_blocks, pl.ds(r0, phase_rows), g * 128:(g + 1) * 128] = picked.astype(BF16)
+
+    def place_last(b):
+        place(pf.at[4 + lax.rem(b, 2)], 2, 1, b)
+
+    kv_q = (qs, ks, vs)
 
     def first(s, carry):
         def project(r, c):
@@ -233,21 +253,22 @@
                 forward_b(0)
 
             rows = hbuf[lax.rem(b, 2)]
-            r0 = pl.multiple_of(r * phase_rows, phase_rows)
-            for n, dst in enumerate((qs, ks, vs)):
+            place_last(jnp.maximum(b - 1, 0))
+            for n in range(3):
                 for i in range(2):
                     res = jnp.dot(rows, wqkv[n, :, i * dim:(i + 1) * dim], preferred_element_type=F32)
                     if n == 0:
                         res = res * scale
+                    piece_no = n * 2 + i
+                    buf = pf.at[4 + lax.rem(b, 2) if piece_no == 5 else piece_no % 4]
                     for g in range(dim // 128):
-                        buf = pf.at[n * 2 + i, g]
-                        buf[...] = res[:, g * 128:(g + 1) * 128]
-                        for ph in range(PHASES):
-                            picked = buf[pl.ds(ph, phase_rows, stride=PHASES), :]
-                            dst[i, SLOT[ph], s, pl.ds(r0, phase_rows), g * 128:(g + 1) * 128] = picked.astype(BF16)
+                        buf[g] = res[:, g * 128:(g + 1) * 128]
+                    if piece_no < 5:
+                        place(buf, n, i, b)
             return c
 
         lax.fori_loop(0, half_blocks, project, 0)
+        place_last((s + 1) * half_blocks - 1)
 
         @pl.when(s == 1)
         def _():
@@ -257,42 +278,16 @@
                     for d in (2, 1):
                         kv3(d, n, i).start()
 
-        def b_pair(i, c):
-            step_b(s, i, far, y, osend.at[2, i, 1 - i, s], ofull.at[y, i, 1 - i, s])
-            step_b(s, i, up, down, osend.at[0, i, 1 - i, s], osend.at[1, i, 1 - i, s])
-            b_relay(s, i).start()
-            for n in range(2):
-                b_direct(n, s, i).start()
-            return c
-
-        lax.fori_loop(0, 2, b_pair, 0)
+        sums = (None, None)
+        for i in range(2):
+            sums = (step_b(s, i, far, y, obuf.at[9, i, 1 - i, s], obuf.at[y, i, 1 - i, s], sums[0]),
+                    step_b(s, i, up, down, obuf.at[8, i, 1 - i, s], obuf.at[4 + y, i, 1 - i, s], sums[1]))
+        for i in range(2):
+            for f in range(4):
+                send_b(f, s, i).start()
         return carry
 
     lax.fori_loop(0, 2, first, 0)
-
-    def outsend(n, i, rows=slice(0, 2 * half)):
-        k = 2 * n + i
-        per = wqkv.shape[1] // (2 * half)
-        return wqkv.at[k // per, pl.ds(pl.multiple_of(lax.rem(k, per) * 2 * half, 2 * half) + rows.start, rows.stop - rows.start), :]
-
-    def u_direct(n, i):
-        return remote(outsend(n, i), out.at[2 * y + i], u_s.at[n, i], u_r.at[n, i], {'tp': dirs[n]})
-
-    def u_relay(i, n):
-        return remote(outsend(2, i, slice(n * half, (n + 1) * half)), orelay.at[i, n], ur_s.at[i, n], ur_r.at[i, n],
-                      {'tp': dirs[n]})
-
-    def u_forward(i, n):
-        return remote(orelay.at[i, n], out.at[2 * near[n] + i, pl.ds(n * half, half)], uf_s.at[i, n], uf_r.at[i, n],
-                      {'tp': dirs[n]})
-
-    def forward_u(i):
-        for n in range(2):
-            u_relay(i, n).wait_recv()
-            u_forward(i, n).start()
-
-    def u_own(i):
-        return pltpu.make_async_copy(outsend(3, i), out.at[2 * y + i], u_loc.at[i])
 
     for k in range(3):
         for n in range(2):
@@ -303,24 +298,34 @@
     def others_first(i, carry):
         for n in range(2):
             kv2(n, i).wait_recv()
-        step_a(far, i, 1, osend.at[2, i, i])
-        a_relay(i).start()
+        step_a(far, i, 1, obuf.at[9, i, i])
+        send_a(1, i).start()
+
+        @pl.when(i == 1)
+        def _():
+            forward_a(0)
+
+        def one(n, c):
+            step_a(lax.rem(y + 1 + 2 * n, tp_size), i, 0, obuf.at[8 + n * (y - 4), i, i])
+
+            @pl.when(n == 0)
+            def _():
+                send_a(0, i).start()
+
+            @pl.when(n == 1)
+            def _():
+                send_a(2, i).start()
+            return c
+
+        lax.fori_loop(0, 2, one, 0)
 
         @pl.when(i == 0)
         def _():
             forward_b(1)
 
-        def one(n, c):
-            step_a(lax.rem(y + 1 + 2 * n, tp_size), i, 0, osend.at[n, i, i])
-            a_direct(n, i).start()
-            return c
-
-        lax.fori_loop(0, 2, one, 0)
         for m in range(2):
             kv3(2, m, i).wait_recv()
             kv3(3, m, i).start()
-        a_relay(i).wait_recv()
-        a_forward(i).start()
         return carry
 
     lax.fori_loop(0, 2, others_first, 0)
@@ -334,55 +339,62 @@
             kv3(1, m, i).wait_recv()
             kv3(3, m, i).wait_recv()
 
-        def own(s, c):
-            step_a(y, i, 2, ofull.at[y, i, i, s], s)
-            return c
-
-        lax.fori_loop(0, 2, own, 0)
-
-        @pl.when(i == 0)
-        def _():
-            for c in wo_local:
-                c.wait()
-            for k in range(3):
-                for j in range(3):
-                    wo_d(j, k).wait_recv()
-                for n in range(2):
-                    wo_df(n, k).wait_recv()
-
         @pl.when(i == 1)
         def _():
-            forward_u(0)
-
-        for n in range(2):
-            a_direct(n, i).wait_recv()
-        a_forward(i).wait_recv()
-        for s in range(2):
-            for n in range(2):
-                b_direct(n, s, 1 - i).wait_recv()
-            b_forward(s, 1 - i).wait_recv()
-        for n, t in ((2, far), (0, up), (1, down), (3, y)):
-            c0 = pl.multiple_of(t * cols, cols)
-            acc = None
-            for src in range(tp_size):
-                for h in range(2):
-                    lhs = ofull[src, h, i].reshape(2 * half, dim)
-                    eighth = slices // 2
-                    rhs = wfull[h * eighth:(h + 1) * eighth, src, :, pl.ds(c0, cols)].reshape(dim, cols)
-                    res = jnp.dot(lhs, rhs, preferred_element_type=F32)
-                    acc = res if acc is None else acc + res
-            outsend(n, i)[...] = acc.astype(BF16)
-            if n == 2:
-                for r in range(2):
-                    u_relay(i, r).start()
-            elif n == 3:
-                u_own(i).start()
-            else:
-                u_direct(n, i).start()
+            forward_a(1)
+
+        def own(s, c):
+            step_a(y, i, 2, obuf.at[y, i, i, s], s)
+            return c
+
+        lax.fori_loop(0, 2, own, 0)
+        send_a(3, i).start()
         return carry
 
     lax.fori_loop(0, 2, own_last, 0)
-    forward_u(1)
+
+    for c in wo_local:
+        c.wait()
+    for k in range(3):
+        for j in range(3):
+            wo_d(j, k).wait_recv()
+        for n in range(2):
+            wo_df(n, k).wait_recv()
+
+    def result(g, kind, i):
+        k = 4 * g + 2 * kind + i
+        per = wqkv.shape[1] // (2 * half)
+        return wqkv.at[k // per, pl.ds(pl.multiple_of(lax.rem(k, per) * 2 * half, 2 * half), 2 * half), :]
+
+    def u_send(g, i):
+        return remote(result(g, 0, i), out.at[2 * (y, down)[g] + i], u_s.at[g, i], u_r.at[g, i],
+                      {'tp': (down, up)[g]})
+
+    def u_own(g, i):
+        return pltpu.make_async_copy(result(g, 1, i), out.at[2 * (y, down)[g] + i], u_loc.at[g, i])
+
+    def project_out(i, carry):
+        for g in range(2):
+            send_a((2, 3)[g], i).wait_recv()
+            pass_a(1 - g, i).wait_recv()
+            for s in range(2):
+                send_b((2, 3)[g], s, 1 - i).wait_recv()
+                pass_b(1 - g, s, 1 - i).wait_recv()
+            for kind, t in enumerate(((down, up)[g], y)):
+                c0 = pl.multiple_of(t * cols, cols)
+                acc = None
+                for src in range(tp_size):
+                    for h in range(2):
+                        lhs = obuf[4 * g + src, h, i].reshape(2 * half, dim)
+                        eighth = slices // 2
+                        rhs = wfull[h * eighth:(h + 1) * eighth, src, :, pl.ds(c0, cols)].reshape(dim, cols)
+                        res = jnp.dot(lhs, rhs, preferred_element_type=F32)
+                        acc = res if acc is None else acc + res
+                result(g, kind, i)[...] = acc.astype(BF16)
+                (u_send, u_own)[kind](g, i).start()
+        return carry
+
+    lax.fori_loop(0, 2, project_out, 0)
 
     for c in wo_y + wo_yf:
         c.wait_send()
@@ -398,18 +410,15 @@
             kv2(n, i).wait_send()
             for d in (1, 2, 3):
                 kv3(d, n, i).wait_send()
-            a_direct(n, i).wait_send()
+            pass_a(n, i).wait_send()
             for s in range(2):
-                b_direct(n, s, i).wait_send()
-            u_direct(n, i).wait()
-            u_relay(i, n).wait_send()
-            u_forward(i, n).wait()
-        a_relay(i).wait_send()
-        a_forward(i).wait_send()
-        for s in range(2):
-            b_relay(s, i).wait_send()
-            b_forward(s, i).wait_send()
-        u_own(i).wait()
+                pass_b(n, s, i).wait_send()
+            u_send(n, i).wait()
+            u_own(n, i).wait()
+        for f in range(4):
+            send_a(f, i).wait_send()
+            for s in range(2):
+                send_b(f, s, i).wait_send()
 
 
 def _natural_order(src, out):
@@ -454,15 +463,13 @@
                 vm(2, PHASES, 2, *tile), vm(2, PHASES, 2, *tile), vm(2, PHASES, 2, *tile),
                 vm(2, 2, 2, *tile), vm(2, 2, 2, *tile), vm(3, 2, 2, *tile), vm(3, 2, 2, *tile),
                 vm(seq_size, head_groups, local_cols // seq_size, model_width),
-                vm(3, 2, 2, 2, *tile), vm(4, 2, 2, 2, *tile), vm(2, 2, *tile), vm(2, 2, *tile),
-                vm(2, 2, half, cols),
+                vm(10, 2, 2, 2, *tile),
                 dma((2,)), dma((3,)), dma((seq_size,)),
                 dma((2,)), dma((2,)), dma((2,)), dma((2,)), dma((2, 3)), dma((2, 3)), dma((2, 3)), dma((2, 3)),
                 dma((3, 3)), dma((3, 3)), dma((2, 3)), dma((2, 3)),
                 dma((2, 2)), dma((2, 2)), dma((3, 2, 2)), dma((3, 2, 2)),
-                dma((2, 2)), dma((2, 2)), dma((2,)), dma((2,)), dma((2,)), dma((2,)),
-                dma((2, 2, 2)), dma((2, 2, 2)), dma((2, 2)), dma((2, 2)), dma((2, 2)), dma((2, 2)),
-                dma((2, 2)), dma((2, 2)), dma((2, 2)), dma((2, 2)), dma((2, 2)), dma((2, 2)), dma((2,)),
+                dma((4, 2)), dma((4, 2)), dma((2, 2)), dma((2, 2)), dma((4, 2, 2)), dma((4, 2, 2)), dma((2, 2, 2)),
+                dma((2, 2, 2)), dma((2, 2)), dma((2, 2)), dma((2, 2)),
             ],
             compiler_params=pltpu.CompilerParams(collective_id=0, has_side_effects=True,
                                                  vmem_limit_bytes=67043328),

time: 146 us -> 138 us (0.945)
  Pallas kernels: 146 us -> 137 us
    pallas_call x1, Pallas kernels: 140 us -> 132 us  [device_fn(): pl.pallas_call(functools.partial(_layer, (block_rows, half, dim, dim ** (...]
where the time goes in v3:
time: 138 us; the launch traced here: 137 us
  Pallas kernels  137 us (99%)
    pallas_call x1, Pallas kernels, device_fn(): pl.pallas_call(functools.partial(_layer, (block_rows, half, dim, dim ** (...  132 us
    pallas_call x1, Pallas kernels, device_fn(): pl.pallas_call(_natural_order, grid=(2 * half // rows,), in_specs=[pl.Blo...  5.54 us

profile of v3, /device:TPU:97, one launch (start us, length us, event | category | flops | bytes accessed | tf_op | source)
XLA Modules:
  0.0 137.4 jit_solution(16336061978352053416)
XLA Ops:
  0.0 131.9 %layer.1.src = bf16[8,512,512]{2,1,0:T(8,128)(2,1)} custom-call(bf16[4096,2048]{1,0:T(8,128)(2,1)} %hidden.1, bf16[2048,512]{1,0:T(8,128)(2,1)} %wq.1, bf16[2048,512]{1,0:T(8,128)(2,1)} %wk.1, bf16[2048,512]{1,0:T(8,128)(2,1)} %wv.1, bf16[512,2048]{1,0:T(8,128)(2,1)} %wo.1, f32[4,8]{1,0:T(4,128)} %bias.1), custom_call_target="tpu_custom_call" | custom-call | tf_op jit(solution)/shard_map/layer/pallas_call | solution.py:455
  131.9 5.5 %natural_order.1 = bf16[4096,512]{1,0:T(8,128)(2,1)} custom-call(bf16[8,512,512]{2,1,0:T(8,128)(2,1)} %layer.1.src), custom_call_target="tpu_custom_call" | custom-call | tf_op jit(solution)/shard_map/natural_order/pallas_call | solution.py:479

commit v4 on v3

--- a/solution.py
+++ b/solution.py
@@ -282,9 +282,10 @@
         for i in range(2):
             sums = (step_b(s, i, far, y, obuf.at[9, i, 1 - i, s], obuf.at[y, i, 1 - i, s], sums[0]),
                     step_b(s, i, up, down, obuf.at[8, i, 1 - i, s], obuf.at[4 + y, i, 1 - i, s], sums[1]))
-        for i in range(2):
-            for f in range(4):
-                send_b(f, s, i).start()
+        for fs in ((0, 1), (2, 3)):
+            for i in range(2):
+                for f in fs:
+                    send_b(f, s, i).start()
         return carry
 
     lax.fori_loop(0, 2, first, 0)
@@ -421,16 +422,29 @@
                 send_b(f, s, i).wait_send()
 
 
-def _natural_order(src, out):
+def _natural_order(src, out, rows_in, rows_out, in_sem, out_sem):
     cols = src.shape[2]
-    group = min(32, src.shape[1])
+    per = src.shape[1] // in_sem.shape[0]
+    group = min(32, per)
     size = group * PHASES
+    loads = [pltpu.make_async_copy(src.at[:, pl.ds(c * per, per), :], rows_in.at[:, pl.ds(c * per, per), :],
+                                   in_sem.at[c]) for c in range(in_sem.shape[0])]
+    stores = [pltpu.make_async_copy(rows_out.at[pl.ds(c * per * PHASES, per * PHASES), :],
+                                    out.at[pl.ds(c * per * PHASES, per * PHASES), :], out_sem.at[c])
+              for c in range(out_sem.shape[0])]
+    for c in loads:
+        c.start()
     to = lax.broadcasted_iota(jnp.int32, (size, size), 0)
     frm = lax.broadcasted_iota(jnp.int32, (size, size), 1)
     perm = jnp.where(frm == lax.rem(to, PHASES) * group + to // PHASES, 1.0, 0.0).astype(BF16)
-    for g in range(src.shape[1] // group):
-        rows = src[:, g * group:(g + 1) * group, :].reshape(size, cols)
-        out[g * size:(g + 1) * size, :] = jnp.dot(perm, rows, preferred_element_type=F32).astype(BF16)
+    for c in range(in_sem.shape[0]):
+        loads[c].wait()
+        for g in range(c * per, (c + 1) * per, group):
+            rows = rows_in[:, g:g + group, :].reshape(size, cols)
+            rows_out[g * PHASES:g * PHASES + size, :] = jnp.dot(perm, rows, preferred_element_type=F32).astype(BF16)
+        stores[c].start()
+    for c in stores:
+        c.wait()
 
 
 def solution(mesh):
@@ -475,13 +489,12 @@
                                                  vmem_limit_bytes=67043328),
             name='layer',
         )(hidden, w_query, w_key, w_value, w_out, branch_bias)
-        rows = min(128, half)
         return pl.pallas_call(
             _natural_order,
-            grid=(2 * half // rows,),
-            in_specs=[pl.BlockSpec((PHASES, rows, cols), lambda b: (0, b, 0))],
-            out_specs=pl.BlockSpec((PHASES * rows, cols), lambda b: (b, 0)),
+            in_specs=[any_spec],
+            out_specs=any_spec,
             out_shape=jax.ShapeDtypeStruct((tokens, cols), BF16),
+            scratch_shapes=[vm(PHASES, 2 * half, cols), vm(tokens, cols), dma((8,)), dma((8,))],
             name='natural_order',
         )(phase_major)
 

time: 138 us -> 137 us (level)
  no operation moved by 1% of the time
where the time goes in v4:
time: 137 us; the launch traced here: 136 us
  Pallas kernels  136 us (99%)
    pallas_call x1, Pallas kernels, device_fn(): pl.pallas_call(functools.partial(_layer, (block_rows, half, dim, dim ** (...  132 us
    pallas_call x1, Pallas kernels, device_fn(): pl.pallas_call(_natural_order, in_specs=[any_spec], out_specs=any_spec, o...  4.41 us

profile of v4, /device:TPU:97, one launch (start us, length us, event | category | flops | bytes accessed | tf_op | source)
XLA Modules:
  0.0 136.5 jit_solution(15817640095241747960)
XLA Ops:
  0.0 131.9 %layer.1.src = bf16[8,512,512]{2,1,0:T(8,128)(2,1)} custom-call(bf16[4096,2048]{1,0:T(8,128)(2,1)} %hidden.1, bf16[2048,512]{1,0:T(8,128)(2,1)} %wq.1, bf16[2048,512]{1,0:T(8,128)(2,1)} %wk.1, bf16[2048,512]{1,0:T(8,128)(2,1)} %wv.1, bf16[512,2048]{1,0:T(8,128)(2,1)} %wo.1, f32[4,8]{1,0:T(4,128)} %bias.1), custom_call_target="tpu_custom_call" | custom-call | tf_op jit(solution)/shard_map/layer/pallas_call | solution.py:469
  131.9 4.4 %natural_order.1 = bf16[4096,512]{1,0:T(8,128)(2,1)} custom-call(bf16[8,512,512]{2,1,0:T(8,128)(2,1)} %layer.1.src), custom_call_target="tpu_custom_call" | custom-call | tf_op jit(solution)/shard_map/natural_order/pallas_call | solution.py:492
